TPU v7x, 32 devices: a whole 2x2x4 slice. The times are simulated.
32 devices in a mesh: groups: 2 (over y), tm: 4 (over z), section: 4 (over x, core).
Axes of the slice: x: 2, y: 2, z: 4, core: 2. Of those that a mesh axis runs over, the one named last changes fastest.
Arguments:
- states: float32 [16, 1, 4096], P(('groups', 'tm')), parts along dimension 0, may hold values from -6 to 6
- timesteps: int32 [16], P(('groups', 'tm')), parts along dimension 0, may hold values from 0 to 999
- step_sizes: float32 [16], P(('groups', 'tm')), parts along dimension 0, may hold values from 0.05 to 0.2
- labels: int32 [2], P('groups'), parts along dimension 0, may hold values from 0 to 1000
- class_table: bfloat16 [1001, 1152], replicated, may hold values from -6 to 6
- embed_weight: bfloat16 [16, 1152], replicated, may hold values from -1.5 to 1.5
- ada_weight: bfloat16 [4, 1152, 2304], P('section', 'tm'), may hold values from -0.1875 to 0.1875
- up_weight: bfloat16 [4, 1152, 2304], P('section', 'tm'), may hold values from -0.1875 to 0.1875
- down_weight: bfloat16 [4, 2304, 1152], P('section', 'tm'), may hold values from -0.125 to 0.125
- final_weight: bfloat16 [1152, 16], replicated, may hold values from -0.1875 to 0.1875
Outputs:
- new_states: float32 [16, 1, 4096], P(('groups', 'tm'), None, 'section'), parts along dimension 0
- step_err: float32 [16], P(('groups', 'tm')), parts along dimension 0
There are 2 independent parts, one for each index of `groups`. A program takes and returns all parts, laid end to end along the dimension named above; an argument that names none is the same for every part. Nothing has to cross between parts.
All inputs are finite; a program needn't handle non-finite values.
Results may differ from a plain program's by a relative error of at most 0.0065.
Values may be sent and summed in bfloat16 or wider, within the bound.
A program may use at most 128 MiB of HBM per device.

v0:
```python
import functools
import math

import jax
import jax.numpy as jnp
from jax import lax
from jax.experimental import pallas as pl
from jax.experimental.pallas import tpu as pltpu
from jax.sharding import PartitionSpec as P

MESH = pl.DeviceIdType.MESH
F32 = jnp.float32
BF16 = jnp.bfloat16


def round_up(value, to):
    return (value + to - 1) // to * to


def pieces_of(columns, limit):
    tiles = columns // 128
    return max(d for d in range(1, limit + 1) if tiles % d == 0)


def worker_of(z, n):
    return z + (1, 0, 0, -1)[z % 4] if n % 4 == 0 else z


def condition_rows(timesteps, labels, class_table):
    width = class_table.shape[1]
    half_width = width // 2
    frequency = jnp.exp(-math.log(10000.0) * jnp.arange(half_width, dtype=F32) / half_width)
    phases = timesteps.astype(F32)[:, None] * frequency[None, :]
    timing = jnp.concatenate([jnp.cos(phases), jnp.sin(phases)], axis=1)
    classes = class_table[labels].astype(F32)
    return jax.nn.silu(timing[:, None, :] + classes[None, :, :]).astype(BF16)


def pad_blocks(array, axis, count, to):
    size = array.shape[axis] // count
    if size == to:
        return array
    shape = array.shape
    array = array.reshape(shape[:axis] + (count, size) + shape[axis + 1 :])
    pads = [(0, 0)] * array.ndim
    pads[axis + 1] = (0, to - size)
    return jnp.pad(array, pads).reshape(shape[:axis] + (count * to,) + shape[axis + 1 :])


def kernel(
    cfg,
    steps_ref,
    cond_ref,
    patch_ref,
    own_ref,
    embed_ref,
    final_ref,
    ada_ref,
    up_ref,
    down_ref,
    new_ref,
    err_ref,
    up_full,
    down_full,
    condw,
    part,
    modw,
    first,
    hbuf,
    xbuf,
    ubuf,
    mod,
    far_patch,
    act,
    leave,
    drift_all,
    drift,
    tot,
    tots,
    errs,
    err_own,
    recv_w,
    send_z,
    send_y,
    local_sem,
    cond_send,
    cond_recv,
    mod_send,
    mod_recv,
    patch_send,
    patch_recv,
    first_send,
    first_recv,
    act_send,
    act_recv,
    dr_send,
    dr_recv,
    tot_send,
    tot_recv,
    err_send,
    err_recv,
):
    n, groups, sections, width, wide, row_count = cfg
    z = lax.axis_index("tm")
    g = lax.axis_index("groups")
    s = lax.axis_index("section")
    steps = patch_ref.shape[0]
    wpad = final_ref.shape[0]
    fpad = up_ref.shape[1]

    barrier = pltpu.get_barrier_semaphore()
    for axis, size, me in (("tm", n, z), ("groups", groups, g), ("section", sections, s)):
        for k in range(1, size):
            pl.semaphore_signal(
                barrier, inc=1, device_id={axis: lax.rem(me + k, size)}, device_id_type=MESH
            )
    paired = n % 4 == 0
    owners = 2 if paired else 1
    side = lax.rem(z, 4)
    if paired:
        works = (side == 1) | (side == 2)
        inward = jnp.where(side == 0, z + 1, z - 1)
        outward = jnp.where(side == 1, z - 1, z + 1)

        @pl.when(jnp.logical_not(works) & (s < sections - 1))
        def _():
            pl.semaphore_signal(
                barrier,
                inc=1,
                device_id={"tm": inward, "section": sections - 1},
                device_id_type=MESH,
            )

    else:
        works = z >= 0
    greeters = (n - 1) + (groups - 1) + (sections - 1)
    if paired:
        greeters = greeters + jnp.where(works & (s == sections - 1), sections - 1, 0)
    pl.semaphore_wait(barrier, greeters)

    def remote(src, dst, ssem, rsem, axis, to):
        return pltpu.make_async_remote_copy(
            src_ref=src,
            dst_ref=dst,
            send_sem=ssem,
            recv_sem=rsem,
            device_id={axis: to},
            device_id_type=MESH,
        )

    def cond_copy(k):
        to = lax.rem(z + k, n)
        return remote(
            cond_ref.at[to], condw.at[z], cond_send.at[k - 1], cond_recv.at[k - 1], "tm", to
        )

    for k in range(1, n):
        cond_copy(k).start()

    def first_copy(k):
        return remote(own_ref.at[0], first, first_send.at[k - 1], first_recv, "tm", k)

    @pl.when(z == 0)
    def _():
        for k in range(1, n):
            first_copy(k).start()

    def patch_copy():
        return remote(patch_ref, far_patch, patch_send, patch_recv, "tm", inward)

    if paired:

        @pl.when(jnp.logical_not(works) & (s == 0))
        def _():
            patch_copy().start()

    shard = (up_ref, down_ref)
    full = (up_full, down_full)
    pieces = recv_w.shape[2]

    def place(w, origin, p):
        rows, columns = shard[w].shape
        size = columns // pieces
        return full[w].at[
            pl.ds(pl.multiple_of(origin * rows, 16), rows), pl.ds(p * size, size)
        ]

    def own_piece(w, p):
        size = shard[w].shape[1] // pieces
        return shard[w].at[:, pl.ds(p * size, size)]

    def along(w, direction, k, p):
        by = 1 - 2 * direction
        origin = z - by * k
        src = own_piece(w, p) if k == 0 else place(w, origin, p)
        return remote(
            src, place(w, origin, p), send_z.at[w, direction, k, p], recv_w.at[w, origin, p], "tm", z + by
        )

    def across(w, direction, k, p, j):
        origin = z - (1 - 2 * direction) * k
        return remote(
            place(w, origin, p),
            place(w, origin, p),
            send_y.at[w, direction, k, p, j - 1],
            recv_w.at[w, origin, p],
            "groups",
            lax.rem(g + j, groups),
        )

    def arrived(w, origin, p):
        return remote(
            place(w, origin, p), place(w, origin, p), send_z.at[w, 0, 0, p], recv_w.at[w, origin, p], "tm", z
        )

    margin = 1 if paired else 0

    def has_next(direction):
        return (z < n - 1 - margin) if direction == 0 else (z > margin)

    def has_origin(direction, k):
        if direction == 0:
            return (z >= k) & (z < n - margin)
        return (z < n - k) & (z >= margin)

    def at_end(direction):
        return (z == 0) if direction == 0 else (z == n - 1)

    def beside_end(direction):
        return (z == 1) if direction == 0 else (z == n - 2)

    for w in range(2):

        @pl.when(g == w % groups)
        def _(w=w):
            for p in range(pieces):
                for direction in range(2):

                    @pl.when(has_next(direction))
                    def _(direction=direction, p=p):
                        along(w, direction, 0, p).start()

    if paired:
        for w in range(2):

            @pl.when(g != w % groups)
            def _(w=w):
                for p in range(pieces):
                    for direction in range(2):

                        @pl.when(at_end(direction))
                        def _(direction=direction, p=p):
                            along(w, direction, 0, p).start()

    def local_copy(w):
        rows = shard[w].shape[0]
        return pltpu.make_async_copy(
            shard[w], full[w].at[pl.ds(pl.multiple_of(z * rows, 16), rows), :], local_sem.at[w]
        )

    for w in range(2):
        local_copy(w).start()

    condw[z] = cond_ref[z]
    for k in range(1, n):
        cond_copy(k).wait()
    pad = condw.shape[1]
    part[...] = jnp.dot(
        condw[...].reshape(n * pad, condw.shape[2]), ada_ref[...], preferred_element_type=F32
    ).reshape(part.shape)

    def slot_of(owner):
        return 0 if worker_of(owner, n) == owner else 1

    def mod_copy(owner):
        slot = slot_of(owner)
        return remote(
            part.at[owner, pl.ds(0, row_count)],
            modw.at[slot, z],
            mod_send.at[owner],
            mod_recv.at[slot, z],
            "tm",
            worker_of(owner, n),
        )

    def mod_arrived(slot, source):
        return remote(
            modw.at[slot, source], modw.at[slot, source], mod_send.at[0], mod_recv.at[slot, source], "tm", z
        )

    for owner in range(n):

        @pl.when(z != worker_of(owner, n))
        def _(owner=owner):
            mod_copy(owner).start()

        @pl.when(z == worker_of(owner, n))
        def _(owner=owner):
            modw[slot_of(owner), z] = part[owner, pl.ds(0, row_count), :]

    for w in range(2):

        @pl.when(g == w % groups)
        def _(w=w):
            for k in range(1, n):
                for p in range(pieces):
                    for direction in range(2):

                        @pl.when(has_origin(direction, k))
                        def _(direction=direction, k=k, p=p):
                            arrived(w, z - (1 - 2 * direction) * k, p).wait_recv()
                            if k < n - 1:

                                @pl.when(has_next(direction))
                                def _():
                                    along(w, direction, k, p).start()

                            for j in range(1, groups):
                                if paired and k == 1:

                                    @pl.when(jnp.logical_not(beside_end(direction)))
                                    def _(j=j):
                                        across(w, direction, k, p, j).start()

                                else:
                                    across(w, direction, k, p, j).start()

    for w in range(2):

        @pl.when(g != w % groups)
        def _(w=w):
            for k in range(1, n):
                for p in range(pieces):
                    for direction in range(2):

                        @pl.when(has_origin(direction, k))
                        def _(direction=direction, k=k, p=p):
                            arrived(w, z - (1 - 2 * direction) * k, p).wait_recv()

    for w in range(2):
        local_copy(w).wait()

    @pl.when(works)
    def _():
        for slot in range(owners):
            total = jnp.zeros(mod.shape[1:], F32)
            for source in range(n):

                @pl.when(z != source)
                def _(slot=slot, source=source):
                    mod_arrived(slot, source).wait_recv()

                total = total + modw[slot, source]
            mod[slot] = total

    block = wpad // n
    real = width // n
    if block != real:
        mask = (lax.broadcasted_iota(jnp.int32, (1, wpad), 1) % block < real).astype(F32)

    def normalize(values):
        center = values - jnp.sum(values, axis=-1, keepdims=True) * (1.0 / width)
        if block != real:
            center = center * mask
        spread = jnp.sum(center * center, axis=-1, keepdims=True) * (1.0 / width)
        return center * lax.rsqrt(spread + 1e-06)

    def act_copy(b):
        return remote(leave.at[b], act.at[b], act_send.at[b], act_recv.at[b], "section", s + 1)

    tile = fpad // 3 if fpad % 768 == 0 else fpad // pieces_of(fpad, 6)
    blocks = owners * steps

    def compute(b):
        slot, step = b // steps, b % steps

        @pl.when(s == 0)
        def _():
            if slot == 1 and step == 0:
                patch_copy().wait_recv()
            tokens = patch_ref[step] if slot == 0 else far_patch[step]
            hbuf[...] = jnp.dot(tokens, embed_ref[...], preferred_element_type=F32)

        @pl.when(s > 0)
        def _():
            act_copy(b).wait_recv()
            hbuf[...] = act[b].astype(F32)

        scale = mod[slot, pl.ds(step, 1), pl.ds(0, wpad)]
        gate = mod[slot, pl.ds(step, 1), pl.ds(wpad, wpad)]
        xbuf[...] = (normalize(hbuf[...]) * (1.0 + scale)).astype(BF16)

        def one(f, carry):
            at = pl.ds(pl.multiple_of(f * tile, tile), tile)
            inner = jnp.dot(xbuf[...], up_full[:, at], preferred_element_type=F32)
            ubuf[:, at] = jax.nn.gelu(inner, approximate=True).astype(BF16)
            return carry

        lax.fori_loop(0, fpad // tile, one, 0)
        branch = jnp.dot(ubuf[...], down_full[...], preferred_element_type=F32)
        leave[b] = (hbuf[...] + gate * branch).astype(BF16)

        @pl.when(s < sections - 1)
        def _():
            act_copy(b).start()

        @pl.when(s == sections - 1)
        def _():
            normed = normalize(leave[b].astype(F32)).astype(BF16)
            drift_all[:, b] = jnp.dot(normed, final_ref[...], preferred_element_type=F32).reshape(
                (sections,) + drift_all.shape[2:]
            )

    order = [b for slot in reversed(range(owners)) for b in range(slot * steps, slot * steps + steps)]

    def drift_copy(slot, d):
        to = {"tm": z if slot == 0 else outward, "section": d}
        return pltpu.make_async_remote_copy(
            src_ref=drift_all.at[d, pl.ds(slot * steps, steps)],
            dst_ref=drift,
            send_sem=dr_send.at[slot, d],
            recv_sem=dr_recv,
            device_id=to,
            device_id_type=MESH,
        )

    @pl.when(works)
    def _():
        for b in order:
            compute(b)
            if b % steps == steps - 1:
                slot = b // steps

                @pl.when(s == sections - 1)
                def _(slot=slot):
                    for d in range(sections if slot else sections - 1):
                        drift_copy(slot, d).start()

    here = works & (s == sections - 1)

    @pl.when(here)
    def _():
        drift[...] = drift_all[sections - 1, pl.ds(0, steps)]

    @pl.when(jnp.logical_not(here))
    def _():
        drift_copy(0, 0).wait_recv()

    running = jnp.zeros(tot.shape, F32)
    for b in range(steps):
        running = running + steps_ref[b] * drift[b]
    tot[...] = running

    def tot_copy(k):
        return remote(tot, tots.at[k - 1], tot_send.at[k - 1], tot_recv.at[k - 1], "tm", z + k)

    for k in range(1, n):

        @pl.when(z < n - k)
        def _(k=k):
            tot_copy(k).start()

    @pl.when(z == 0)
    def _():
        first[...] = own_ref[0]

    @pl.when(z > 0)
    def _():
        first_copy(1).wait_recv()

    tot_start = first[...]
    new_ref[0] = jnp.zeros(tot.shape, F32)
    for k in range(n - 1, 0, -1):

        @pl.when(z >= k)
        def _(k=k):
            tot_copy(k).wait_recv()
            new_ref[0] = new_ref[0] + tots[k - 1]

    base = tot_start + new_ref[0]
    running = jnp.zeros(tot.shape, F32)
    errors = []
    for b in range(steps):
        fresh = base + running
        running = running + steps_ref[b] * drift[b]
        new_ref[b] = fresh
        delta = jnp.max(jnp.abs(fresh - own_ref[b]), axis=0, keepdims=True)
        errors.append(jnp.broadcast_to(jnp.max(delta, axis=1, keepdims=True), (1, 128)))
    for b in range(steps):
        err_own[pl.ds(b, 1), :] = errors[b]
    for b in range(steps, err_own.shape[0]):
        err_own[pl.ds(b, 1), :] = jnp.zeros((1, 128), F32)

    def err_copy(k):
        return remote(
            err_own, errs.at[k - 1], err_send.at[k - 1], err_recv.at[k - 1], "section", lax.rem(s + k, sections)
        )

    for k in range(1, sections):
        err_copy(k).start()
    worst = err_own[...]
    for k in range(1, sections):
        err_copy(k).wait()
        worst = jnp.maximum(worst, errs[k - 1])
    err_ref[...] = worst

    @pl.when(z == 0)
    def _():
        for k in range(1, n):
            first_copy(k).wait_send()

    for w in range(2):

        @pl.when(g == w % groups)
        def _(w=w):
            for k in range(n):
                for p in range(pieces):
                    for direction in range(2):

                        @pl.when(has_origin(direction, k))
                        def _(direction=direction, k=k, p=p):
                            if k < n - 1:

                                @pl.when(has_next(direction))
                                def _():
                                    along(w, direction, k, p).wait_send()

                            if k > 0:
                                for j in range(1, groups):
                                    if paired and k == 1:

                                        @pl.when(jnp.logical_not(beside_end(direction)))
                                        def _(j=j):
                                            across(w, direction, k, p, j).wait_send()

                                    else:
                                        across(w, direction, k, p, j).wait_send()

    for owner in range(n):

        @pl.when(z != worker_of(owner, n))
        def _(owner=owner):
            mod_copy(owner).wait_send()

    if paired:
        for w in range(2):

            @pl.when(g != w % groups)
            def _(w=w):
                for p in range(pieces):
                    for direction in range(2):

                        @pl.when(at_end(direction))
                        def _(direction=direction, p=p):
                            along(w, direction, 0, p).wait_send()

        @pl.when(jnp.logical_not(works) & (s == 0))
        def _():
            patch_copy().wait_send()

    @pl.when(works & (s < sections - 1))
    def _():
        for b in range(blocks):
            act_copy(b).wait_send()

    @pl.when(here)
    def _():
        for slot in range(owners):
            for d in range(sections if slot else sections - 1):
                drift_copy(slot, d).wait_send()

    for k in range(1, n):

        @pl.when(z < n - k)
        def _(k=k):
            tot_copy(k).wait_send()


def shards(
    sizes,
    states,
    timesteps,
    step_sizes,
    labels,
    class_table,
    embed_weight,
    ada_weight,
    up_weight,
    down_weight,
    final_weight,
):
    n, groups, sections = sizes
    steps, batch, p_size = states.shape
    channels, width = embed_weight.shape
    wide = up_weight.shape[2]
    patches = p_size // channels
    own_patches = patches // sections
    block = round_up(width // n, 16)
    wide_block = round_up(wide // n, 16)
    wpad, fpad = n * block, n * wide_block
    pad = 16
    row_count = 8
    owners = 2 if n % 4 == 0 else 1
    blocks = owners * steps

    cond = condition_rows(timesteps, labels, class_table).reshape(steps, n, width // n)
    cond = jnp.pad(cond.transpose(1, 0, 2), ((0, 0), (0, pad - steps), (0, 0)))
    tokens = states.reshape(steps, patches, channels)
    own = lax.dynamic_slice_in_dim(tokens, lax.axis_index("section") * own_patches, own_patches, 1)
    embed = pad_blocks(embed_weight, 1, n, block)
    final = pad_blocks(final_weight, 0, n, block)
    ada = pad_blocks(ada_weight[0], 1, 2 * n, block)
    up = pad_blocks(pad_blocks(up_weight[0], 1, n, wide_block), 0, 1, block)
    down = pad_blocks(pad_blocks(down_weight[0], 1, n, block), 0, 1, wide_block)
    limit = max(1, 36 // n)
    pieces = max(
        d for d in range(1, limit + 1) if (wpad // 128) % d == 0 and (fpad // 128) % d == 0
    )
    vmem = pltpu.VMEM
    dma = pltpu.SemaphoreType.DMA
    part_shape = (steps, own_patches, channels)
    new_states, errors = pl.pallas_call(
        functools.partial(kernel, (n, groups, sections, width, wide, row_count)),
        out_shape=(
            jax.ShapeDtypeStruct(part_shape, F32),
            jax.ShapeDtypeStruct((8, 128), F32),
        ),
        in_specs=[pl.BlockSpec(memory_space=pltpu.SMEM)] + [pl.BlockSpec(memory_space=vmem)] * 8,
        out_specs=(pl.BlockSpec(memory_space=vmem), pl.BlockSpec(memory_space=vmem)),
        scratch_shapes=[
            vmem((wpad, fpad), BF16),
            vmem((fpad, wpad), BF16),
            vmem((n, pad, width // n), BF16),
            vmem((n, pad, 2 * wpad), F32),
            vmem((owners, n, row_count, 2 * wpad), F32),
            vmem(part_shape[1:], F32),
            vmem((patches, wpad), F32),
            vmem((patches, wpad), BF16),
            vmem((patches, fpad), BF16),
            vmem((owners, row_count, 2 * wpad), F32),
            vmem((steps, patches, channels), BF16),
            vmem((blocks, patches, wpad), BF16),
            vmem((blocks, patches, wpad), BF16),
            vmem((sections, blocks, own_patches, channels), F32),
            vmem(part_shape, F32),
            vmem(part_shape[1:], F32),
            vmem((max(n - 1, 1),) + part_shape[1:], F32),
            vmem((max(sections - 1, 1), 8, 128), F32),
            vmem((8, 128), F32),
            dma((2, n, pieces)),
            dma((2, 2, n, pieces)),
            dma((2, 2, n, pieces, max(groups - 1, 1))),
            dma((2,)),
            dma((n,)),
            dma((n,)),
            dma((n,)),
            dma((owners, n)),
            dma(()),
            dma(()),
            dma((n,)),
            dma(()),
            dma((blocks,)),
            dma((blocks,)),
            dma((owners, sections)),
            dma(()),
            dma((n,)),
            dma((n,)),
            dma((sections,)),
            dma((sections,)),
        ],
        compiler_params=pltpu.CompilerParams(
            collective_id=0, has_side_effects=True, vmem_limit_bytes=60 * 1024 * 1024
        ),
    )(step_sizes, cond, tokens.astype(BF16), own, embed, final, ada, up, down)
    return new_states.reshape(steps, batch, p_size // sections), errors[:steps, 0]


def solution(mesh):
    sizes = (mesh.shape["tm"], mesh.shape["groups"], mesh.shape["section"])
    return jax.shard_map(
        functools.partial(shards, sizes),
        mesh=mesh,
        in_specs=(
            P(("groups", "tm"), None, None),
            P(("groups", "tm")),
            P(("groups", "tm")),
            P("groups"),
            P(),
            P(),
            P("section", "tm", None),
            P("section", "tm", None),
            P("section", "tm", None),
            P(),
        ),
        out_specs=(P(("groups", "tm"), None, "section"), P(("groups", "tm"))),
        check_vma=False,
    )
```

profile of v0, /device:TPU:27, one launch (start us, length us, event | category | flops | bytes accessed | tf_op | source)
XLA Modules:
  0.0 147.7 jit_solution(6715052011853783675)
XLA Ops:
  1.3 0.7 convert_element_type.26
  2.0 0.2 multiply_cosine_fusion
  2.1 0.1 pad_maximum_fusion
  2.2 0.1 concatenate.7
  2.3 0.8 convert_reduce_fusion
  3.0 0.1 reshape.119
  3.2 0.9 reduce.1
  4.0 0.6 pad.4.cond_ref
  4.7 0.1 reshape.98
  4.8 0.6 constant_dynamic-slice_fusion.own_ref
  5.4 0.7 convert_element_type.30.patch_ref
  6.1 1.6 %copy.19.final_ref = bf16[1152,16]{1,0:T(8,128)(2,1)} copy(bf16[1152,16]{0,1:T(8,128)(2,1)} %param.19) | data formatting | bytes 73728 | tf_op args[9]
  7.7 137.1 %shard_map.113 = (f32[2,64,16]{2,1,0:T(8,128)}, f32[8,128]{1,0:T(8,128)}) custom-call(f32[2]{0:T(128)} %steps_ref.1, bf16[4,16,288]{2,1,0:T(8,128)(2,1)} %pad.4.cond_ref, bf16[2,256,16]{2,1,0:T(8,128)(2,1)} %convert_element_type.30.patch_ref, f32[2,64,16]{2,1,0:T(8,128)} %constant_dynamic-slice_fusion.own_ref, bf16[16,1152]{1,0:T(8,128)(2,1)} %embed_ref.1, ...), custom_call_target="tpu_custom_call" | custom-call | tf_op jit(solution)/shard_map/pallas_call | solution.py:622
  144.9 1.5 %reshape.121 = f32[2,1,1024]{2,1,0:T(1,128)} reshape(f32[2,64,16]{2,1,0:T(8,128)} %get-tuple-element.4) | data formatting | bytes 16384 | tf_op jit(solution)/shard_map/reshape | solution.py:675
  146.4 1.3 slice_reduce_fusion
  (4 shorter events, 0.0 us)
where the time goes:
time: 148 us
  Pallas kernels  137 us (93%)
  local copies, waits for them, and re-layouts  6.05 us (4%)
  other arithmetic  3.21 us (2%)
    pallas_call x1, Pallas kernels, shards(): pl.pallas_call(functools.partial(kernel, (n, groups, sections, width, wid...  137 us

commit v1 on v0

--- a/solution.py
+++ b/solution.py
@@ -11,6 +11,8 @@
 MESH = pl.DeviceIdType.MESH
 F32 = jnp.float32
 BF16 = jnp.bfloat16
+CORES = 2
+LAG = 2
 
 
 def round_up(value, to):
@@ -51,7 +53,7 @@
     cfg,
     steps_ref,
     cond_ref,
-    patch_ref,
+    tokens_ref,
     own_ref,
     embed_ref,
     final_ref,
@@ -70,7 +72,7 @@
     xbuf,
     ubuf,
     mod,
-    far_patch,
+    tok,
     act,
     leave,
     drift_all,
@@ -99,12 +101,14 @@
     tot_recv,
     err_send,
     err_recv,
+    go,
 ):
-    n, groups, sections, width, wide, row_count = cfg
+    n, groups, sections, width = cfg
     z = lax.axis_index("tm")
     g = lax.axis_index("groups")
     s = lax.axis_index("section")
-    steps = patch_ref.shape[0]
+    steps = own_ref.shape[0]
+    patches, channels = tokens_ref.shape[0] // steps, tokens_ref.shape[1]
     wpad = final_ref.shape[0]
     fpad = up_ref.shape[1]
 
@@ -166,7 +170,9 @@
             first_copy(k).start()
 
     def patch_copy():
-        return remote(patch_ref, far_patch, patch_send, patch_recv, "tm", inward)
+        return remote(
+            tokens_ref, tok.at[pl.ds(steps * patches, steps * patches)], patch_send, patch_recv, "tm", inward
+        )
 
     if paired:
 
@@ -177,6 +183,17 @@
     shard = (up_ref, down_ref)
     full = (up_full, down_full)
     pieces = recv_w.shape[2]
+    sets = [range(at, min(at + groups, pieces)) for at in range(0, pieces, groups)]
+    blocks = owners * steps
+    cut = 2 if sections % 2 == 0 else 1
+    units, span = blocks * cut, patches // cut
+    early = min(CORES, sections - 1)
+    leads = lax.rem(s, CORES) == 0
+    margin = 1 if paired else 0
+    last = n - 1 - margin
+
+    def owner_of(w, p):
+        return (w + p) % groups
 
     def place(w, origin, p):
         rows, columns = shard[w].shape
@@ -213,8 +230,6 @@
             place(w, origin, p), place(w, origin, p), send_z.at[w, 0, 0, p], recv_w.at[w, origin, p], "tm", z
         )
 
-    margin = 1 if paired else 0
-
     def has_next(direction):
         return (z < n - 1 - margin) if direction == 0 else (z > margin)
 
@@ -229,28 +244,74 @@
     def beside_end(direction):
         return (z == 1) if direction == 0 else (z == n - 2)
 
-    for w in range(2):
-
-        @pl.when(g == w % groups)
-        def _(w=w):
-            for p in range(pieces):
-                for direction in range(2):
-
-                    @pl.when(has_next(direction))
-                    def _(direction=direction, p=p):
-                        along(w, direction, 0, p).start()
-
-    if paired:
-        for w in range(2):
-
-            @pl.when(g != w % groups)
-            def _(w=w):
-                for p in range(pieces):
+    def own_sends(w, members, act_on):
+        for case in range(groups):
+
+            @pl.when(g == case)
+            def _(case=case):
+                for p in sorted(members, key=lambda p: owner_of(w, p) != case):
+                    mine = owner_of(w, p) == case
                     for direction in range(2):
-
-                        @pl.when(at_end(direction))
-                        def _(direction=direction, p=p):
-                            along(w, direction, 0, p).start()
+                        if mine or paired:
+
+                            @pl.when(has_next(direction) if mine else at_end(direction))
+                            def _(direction=direction, p=p):
+                                act_on(along(w, direction, 0, p))
+
+    def start(copy):
+        copy.start()
+
+    def wait_send(copy):
+        copy.wait_send()
+
+    runs = [(w, members) for w in range(2) for members in sets]
+    ahead = min(3, len(runs))
+
+    def send_first():
+        for at, (w, members) in enumerate(runs):
+            if at < ahead:
+                own_sends(w, members, start)
+
+    def relay(w, k, members):
+        for case in range(groups):
+
+            @pl.when(g == case)
+            def _(case=case):
+                for p in members:
+                    if owner_of(w, p) == case:
+                        for direction in range(2):
+
+                            @pl.when(has_origin(direction, k))
+                            def _(direction=direction, p=p):
+                                arrived(w, z - (1 - 2 * direction) * k, p).wait_recv()
+
+                                @pl.when(has_next(direction))
+                                def _():
+                                    along(w, direction, k, p).start()
+
+                                for j in range(1, groups):
+                                    if paired and k == 1:
+
+                                        @pl.when(jnp.logical_not(beside_end(direction)))
+                                        def _(j=j):
+                                            across(w, direction, k, p, j).start()
+
+                                    else:
+                                        across(w, direction, k, p, j).start()
+
+    def rest_arrived(w, members):
+        for case in range(groups):
+
+            @pl.when(g == case)
+            def _(case=case):
+                for p in members:
+                    if owner_of(w, p) != case:
+                        for k in range(1, last + 1):
+                            for direction in range(2):
+
+                                @pl.when(has_origin(direction, k))
+                                def _(direction=direction, k=k, p=p):
+                                    arrived(w, z - (1 - 2 * direction) * k, p).wait_recv()
 
     def local_copy(w):
         rows = shard[w].shape[0]
@@ -258,6 +319,13 @@
             shard[w], full[w].at[pl.ds(pl.multiple_of(z * rows, 16), rows), :], local_sem.at[w]
         )
 
+    ends = at_end(0) | at_end(1) if paired else z < 0
+    led = leads & (s < sections - 1)
+
+    @pl.when(leads)
+    def _():
+        send_first()
+
     for w in range(2):
         local_copy(w).start()
 
@@ -265,9 +333,11 @@
     for k in range(1, n):
         cond_copy(k).wait()
     pad = condw.shape[1]
-    part[...] = jnp.dot(
+    products = jnp.dot(
         condw[...].reshape(n * pad, condw.shape[2]), ada_ref[...], preferred_element_type=F32
-    ).reshape(part.shape)
+    )
+    for owner in range(n):
+        part[owner] = products[owner * pad : owner * pad + steps]
 
     def slot_of(owner):
         return 0 if worker_of(owner, n) == owner else 1
@@ -275,7 +345,7 @@
     def mod_copy(owner):
         slot = slot_of(owner)
         return remote(
-            part.at[owner, pl.ds(0, row_count)],
+            part.at[owner],
             modw.at[slot, z],
             mod_send.at[owner],
             mod_recv.at[slot, z],
@@ -296,62 +366,20 @@
 
         @pl.when(z == worker_of(owner, n))
         def _(owner=owner):
-            modw[slot_of(owner), z] = part[owner, pl.ds(0, row_count), :]
-
-    for w in range(2):
-
-        @pl.when(g == w % groups)
-        def _(w=w):
-            for k in range(1, n):
-                for p in range(pieces):
-                    for direction in range(2):
-
-                        @pl.when(has_origin(direction, k))
-                        def _(direction=direction, k=k, p=p):
-                            arrived(w, z - (1 - 2 * direction) * k, p).wait_recv()
-                            if k < n - 1:
-
-                                @pl.when(has_next(direction))
-                                def _():
-                                    along(w, direction, k, p).start()
-
-                            for j in range(1, groups):
-                                if paired and k == 1:
-
-                                    @pl.when(jnp.logical_not(beside_end(direction)))
-                                    def _(j=j):
-                                        across(w, direction, k, p, j).start()
-
-                                else:
-                                    across(w, direction, k, p, j).start()
-
-    for w in range(2):
-
-        @pl.when(g != w % groups)
-        def _(w=w):
-            for k in range(1, n):
-                for p in range(pieces):
-                    for direction in range(2):
-
-                        @pl.when(has_origin(direction, k))
-                        def _(direction=direction, k=k, p=p):
-                            arrived(w, z - (1 - 2 * direction) * k, p).wait_recv()
-
-    for w in range(2):
-        local_copy(w).wait()
-
-    @pl.when(works)
-    def _():
-        for slot in range(owners):
-            total = jnp.zeros(mod.shape[1:], F32)
-            for source in range(n):
-
-                @pl.when(z != source)
-                def _(slot=slot, source=source):
-                    mod_arrived(slot, source).wait_recv()
-
-                total = total + modw[slot, source]
-            mod[slot] = total
+            modw[slot_of(owner), z] = part[owner]
+
+    @pl.when(jnp.logical_not(leads))
+    def _():
+        pl.semaphore_wait(go, 1)
+        send_first()
+
+    @pl.when(ends)
+    def _():
+        for w, members in runs[ahead:]:
+            own_sends(w, members, start)
+
+    def release():
+        pl.semaphore_signal(go, inc=1, device_id={"section": s + 1}, device_id_type=MESH)
 
     block = wpad // n
     real = width // n
@@ -365,56 +393,162 @@
         spread = jnp.sum(center * center, axis=-1, keepdims=True) * (1.0 / width)
         return center * lax.rsqrt(spread + 1e-06)
 
-    def act_copy(b):
-        return remote(leave.at[b], act.at[b], act_send.at[b], act_recv.at[b], "section", s + 1)
-
-    tile = fpad // 3 if fpad % 768 == 0 else fpad // pieces_of(fpad, 6)
-    blocks = owners * steps
-
-    def compute(b):
-        slot, step = b // steps, b % steps
-
+    everything = pl.ds(0, units * span)
+
+    def act_copy(u, at=None, rows=None):
+        rows = pl.ds(pl.multiple_of(u * span, span), span) if rows is None else rows
+        window = (rows, pl.ds(0, wpad) if at is None else at)
+        return remote(leave.at[window], act.at[window], act_send.at[u], act_recv.at[u], "section", s + 1)
+
+    def turn(i):
+        return lax.rem(i + (owners - 1) * steps * cut, units)
+
+    def modulations():
+        for slot in range(owners):
+            total = jnp.zeros(modw.shape[2:], F32)
+            for source in range(n):
+
+                @pl.when(z != source)
+                def _(slot=slot, source=source):
+                    mod_arrived(slot, source).wait_recv()
+
+                total = total + modw[slot, source]
+            for step in range(steps):
+                mod[slot * steps + step] = total[step : step + 1]
+
+    def scaled(b, values):
+        return (normalize(values) * (1.0 + mod[b, :, pl.ds(0, wpad)])).astype(BF16)
+
+    def prepare():
         @pl.when(s == 0)
         def _():
-            if slot == 1 and step == 0:
+            tok[pl.ds(0, steps * patches)] = tokens_ref[...]
+            if paired:
                 patch_copy().wait_recv()
-            tokens = patch_ref[step] if slot == 0 else far_patch[step]
-            hbuf[...] = jnp.dot(tokens, embed_ref[...], preferred_element_type=F32)
 
         @pl.when(s > 0)
         def _():
-            act_copy(b).wait_recv()
-            hbuf[...] = act[b].astype(F32)
-
-        scale = mod[slot, pl.ds(step, 1), pl.ds(0, wpad)]
-        gate = mod[slot, pl.ds(step, 1), pl.ds(wpad, wpad)]
-        xbuf[...] = (normalize(hbuf[...]) * (1.0 + scale)).astype(BF16)
-
-        def one(f, carry):
-            at = pl.ds(pl.multiple_of(f * tile, tile), tile)
-            inner = jnp.dot(xbuf[...], up_full[:, at], preferred_element_type=F32)
-            ubuf[:, at] = jax.nn.gelu(inner, approximate=True).astype(BF16)
+            act_copy(0, rows=everything).wait_recv()
+
+        def one(b, carry):
+            rows = pl.ds(pl.multiple_of(b * patches, patches), patches)
+
+            @pl.when(s == 0)
+            def _():
+                hbuf[...] = jnp.dot(tok[rows], embed_ref[...], preferred_element_type=F32)
+
+            @pl.when(s > 0)
+            def _():
+                hbuf[...] = act[rows].astype(F32)
+
+            xbuf[rows] = scaled(b, hbuf[...])
             return carry
 
-        lax.fori_loop(0, fpad // tile, one, 0)
-        branch = jnp.dot(ubuf[...], down_full[...], preferred_element_type=F32)
-        leave[b] = (hbuf[...] + gate * branch).astype(BF16)
-
-        @pl.when(s < sections - 1)
-        def _():
-            act_copy(b).start()
-
-        @pl.when(s == sections - 1)
-        def _():
-            normed = normalize(leave[b].astype(F32)).astype(BF16)
-            drift_all[:, b] = jnp.dot(normed, final_ref[...], preferred_element_type=F32).reshape(
-                (sections,) + drift_all.shape[2:]
-            )
-
-    order = [b for slot in reversed(range(owners)) for b in range(slot * steps, slot * steps + steps)]
+        lax.fori_loop(0, blocks, one, 0)
+
+    def columns_of(w, members):
+        size = shard[w].shape[1] // pieces
+        return pl.ds(members[0] * size, len(members) * size)
+
+    def gelu(values):
+        return jax.nn.gelu(values, approximate=True).astype(BF16)
+
+    def early_up(members):
+        at = columns_of(0, members)
+        ubuf[:, at] = gelu(jnp.dot(xbuf[...], up_full[:, at], preferred_element_type=F32))
+
+    def early_down(members):
+        at = columns_of(1, members)
+        branch = jnp.dot(ubuf[...], down_full[:, at], preferred_element_type=F32)
+
+        def combine(before):
+            for b in range(blocks):
+                rows = pl.ds(b * patches, patches)
+                gate = mod[b, :, pl.ds(wpad + at.start, at.size)]
+                here = gate * branch[b * patches : (b + 1) * patches]
+                leave[rows, at] = (before(rows) + here).astype(BF16)
+
+        @pl.when(s == 0)
+        def _():
+            combine(lambda rows: jnp.dot(tok[rows], embed_ref[:, at], preferred_element_type=F32))
+
+        @pl.when(s > 0)
+        def _():
+            combine(lambda rows: act[rows, at].astype(F32))
+
+        @pl.when(s + 1 < early)
+        def _():
+            act_copy(0, at, everything).start()
+
+        @pl.when(s + 1 == early)
+        def _():
+            for i in range(units // 2):
+                act_copy(turn(i), at).start()
+
+    streams = works & (s < early)
+    count = len(sets)
+    begin = min(3, 2 * count - 1)
+    behind = LAG * (last - 1) + 1
+    expands = [max(j + behind, begin + 1 + j // 2) for j in range(count)]
+    tasks = [(begin, prepare, None)]
+    tasks += [(t, early_up, (0, members)) for t, members in zip(expands, sets)]
+    tasks += [
+        (max(count + j + behind, expands[-1]), early_down, (1, members)) for j, members in enumerate(sets)
+    ]
+
+    def do(task):
+        _, work, run = task
+        if run is not None:
+            rest_arrived(*run)
+
+        @pl.when(streams)
+        def _():
+            if run is None:
+                modulations()
+                work()
+            else:
+                work(run[1])
+
+    for w in range(2):
+        local_copy(w).wait()
+
+    @pl.when(led & ends)
+    def _():
+        for w, members in runs[:-1]:
+            own_sends(w, members, wait_send)
+        release()
+
+    for t in range(len(runs) + LAG * (last - 1)):
+        if t + ahead < len(runs):
+
+            @pl.when(jnp.logical_not(ends))
+            def _(t=t):
+                own_sends(*runs[t + ahead], start)
+
+        for k in range(1, last + 1):
+            if 0 <= t - LAG * (k - 1) < len(runs):
+                w, members = runs[t - LAG * (k - 1)]
+                relay(w, k, members)
+        if t == len(runs) - 1:
+
+            @pl.when(led & jnp.logical_not(ends))
+            def _():
+                release()
+
+        for task in tasks:
+            if task[0] == t:
+                do(task)
+    for task in tasks:
+        if task[0] >= len(runs) + LAG * (last - 1):
+            do(task)
+
+    @pl.when(streams & (s + 1 == early))
+    def _():
+        for i in range(units // 2, units):
+            act_copy(turn(i)).start()
 
     def drift_copy(slot, d):
-        to = {"tm": z if slot == 0 else outward, "section": d}
+        to = {"tm": jnp.where(slot == 0, z, outward) if paired else z, "section": d}
         return pltpu.make_async_remote_copy(
             src_ref=drift_all.at[d, pl.ds(slot * steps, steps)],
             dst_ref=drift,
@@ -424,17 +558,51 @@
             device_id_type=MESH,
         )
 
-    @pl.when(works)
-    def _():
-        for b in order:
-            compute(b)
-            if b % steps == steps - 1:
-                slot = b // steps
-
-                @pl.when(s == sections - 1)
-                def _(slot=slot):
-                    for d in range(sections if slot else sections - 1):
-                        drift_copy(slot, d).start()
+    tile = 256 if fpad % 256 == 0 else 128
+
+    @pl.when(works & (s >= early))
+    def _():
+        modulations()
+
+        def one(i, carry):
+            u = turn(i)
+            b, part_of = u // cut, lax.rem(u, cut)
+            rows = pl.ds(pl.multiple_of(u * span, span), span)
+            act_copy(u).wait_recv()
+            x = scaled(b, act[rows].astype(F32))
+            before = None
+            for at in range(0, fpad, tile):
+                inner = jnp.dot(x, up_full[:, at : at + tile], preferred_element_type=F32)
+                if before is not None:
+                    ubuf[rows, at - tile : at] = gelu(before)
+                before = inner
+            ubuf[rows, fpad - tile : fpad] = gelu(before)
+            branch = jnp.dot(ubuf[rows], down_full[...], preferred_element_type=F32)
+            result = (act[rows].astype(F32) + mod[b, :, pl.ds(wpad, wpad)] * branch).astype(BF16)
+
+            @pl.when(s < sections - 1)
+            def _():
+                leave[rows] = result
+                act_copy(u).start()
+
+            @pl.when(s == sections - 1)
+            def _():
+                normed = normalize(result.astype(F32)).astype(BF16)
+                fresh = jnp.dot(normed, final_ref[...], preferred_element_type=F32)
+                share = sections // cut
+                drift_all[pl.ds(part_of * share, share), b] = fresh.reshape(
+                    (share,) + drift_all.shape[2:]
+                )
+                for slot in range(owners):
+
+                    @pl.when(u == ((slot + 1) * steps) * cut - 1)
+                    def _(slot=slot):
+                        for d in range(sections if slot else sections - 1):
+                            drift_copy(slot, d).start()
+
+            return carry
+
+        lax.fori_loop(0, units, one, 0)
 
     here = works & (s == sections - 1)
 
@@ -509,32 +677,38 @@
         for k in range(1, n):
             first_copy(k).wait_send()
 
+    @pl.when(jnp.logical_not(led & ends))
+    def _():
+        for w, members in runs[:-1]:
+            own_sends(w, members, wait_send)
+
+    for w, members in runs[-1:]:
+        own_sends(w, members, wait_send)
     for w in range(2):
-
-        @pl.when(g == w % groups)
-        def _(w=w):
-            for k in range(n):
-                for p in range(pieces):
-                    for direction in range(2):
-
-                        @pl.when(has_origin(direction, k))
-                        def _(direction=direction, k=k, p=p):
-                            if k < n - 1:
-
-                                @pl.when(has_next(direction))
-                                def _():
-                                    along(w, direction, k, p).wait_send()
-
-                            if k > 0:
-                                for j in range(1, groups):
-                                    if paired and k == 1:
-
-                                        @pl.when(jnp.logical_not(beside_end(direction)))
-                                        def _(j=j):
+        for k in range(1, last + 1):
+            for case in range(groups):
+
+                @pl.when(g == case)
+                def _(w=w, k=k, case=case):
+                    for p in range(pieces):
+                        if owner_of(w, p) == case:
+                            for direction in range(2):
+
+                                @pl.when(has_origin(direction, k))
+                                def _(direction=direction, p=p):
+                                    @pl.when(has_next(direction))
+                                    def _():
+                                        along(w, direction, k, p).wait_send()
+
+                                    for j in range(1, groups):
+                                        if paired and k == 1:
+
+                                            @pl.when(jnp.logical_not(beside_end(direction)))
+                                            def _(j=j):
+                                                across(w, direction, k, p, j).wait_send()
+
+                                        else:
                                             across(w, direction, k, p, j).wait_send()
-
-                                    else:
-                                        across(w, direction, k, p, j).wait_send()
 
     for owner in range(n):
 
@@ -543,16 +717,6 @@
             mod_copy(owner).wait_send()
 
     if paired:
-        for w in range(2):
-
-            @pl.when(g != w % groups)
-            def _(w=w):
-                for p in range(pieces):
-                    for direction in range(2):
-
-                        @pl.when(at_end(direction))
-                        def _(direction=direction, p=p):
-                            along(w, direction, 0, p).wait_send()
 
         @pl.when(jnp.logical_not(works) & (s == 0))
         def _():
@@ -560,8 +724,14 @@
 
     @pl.when(works & (s < sections - 1))
     def _():
-        for b in range(blocks):
-            act_copy(b).wait_send()
+        @pl.when(s + 1 < early)
+        def _():
+            act_copy(0, rows=everything).wait_send()
+
+        @pl.when(s + 1 >= early)
+        def _():
+            for u in range(units):
+                act_copy(u).wait_send()
 
     @pl.when(here)
     def _():
@@ -599,9 +769,9 @@
     wide_block = round_up(wide // n, 16)
     wpad, fpad = n * block, n * wide_block
     pad = 16
-    row_count = 8
     owners = 2 if n % 4 == 0 else 1
     blocks = owners * steps
+    units = blocks * (2 if sections % 2 == 0 else 1)
 
     cond = condition_rows(timesteps, labels, class_table).reshape(steps, n, width // n)
     cond = jnp.pad(cond.transpose(1, 0, 2), ((0, 0), (0, pad - steps), (0, 0)))
@@ -620,7 +790,7 @@
     dma = pltpu.SemaphoreType.DMA
     part_shape = (steps, own_patches, channels)
     new_states, errors = pl.pallas_call(
-        functools.partial(kernel, (n, groups, sections, width, wide, row_count)),
+        functools.partial(kernel, (n, groups, sections, width)),
         out_shape=(
             jax.ShapeDtypeStruct(part_shape, F32),
             jax.ShapeDtypeStruct((8, 128), F32),
@@ -631,16 +801,16 @@
             vmem((wpad, fpad), BF16),
             vmem((fpad, wpad), BF16),
             vmem((n, pad, width // n), BF16),
-            vmem((n, pad, 2 * wpad), F32),
-            vmem((owners, n, row_count, 2 * wpad), F32),
+            vmem((n, steps, 2 * wpad), F32),
+            vmem((owners, n, steps, 2 * wpad), F32),
             vmem(part_shape[1:], F32),
             vmem((patches, wpad), F32),
-            vmem((patches, wpad), BF16),
-            vmem((patches, fpad), BF16),
-            vmem((owners, row_count, 2 * wpad), F32),
-            vmem((steps, patches, channels), BF16),
-            vmem((blocks, patches, wpad), BF16),
-            vmem((blocks, patches, wpad), BF16),
+            vmem((blocks * patches, wpad), BF16),
+            vmem((blocks * patches, fpad), BF16),
+            vmem((blocks, 1, 2 * wpad), F32),
+            vmem((blocks * patches, channels), BF16),
+            vmem((blocks * patches, wpad), BF16),
+            vmem((blocks * patches, wpad), BF16),
             vmem((sections, blocks, own_patches, channels), F32),
             vmem(part_shape, F32),
             vmem(part_shape[1:], F32),
@@ -659,19 +829,20 @@
             dma(()),
             dma((n,)),
             dma(()),
-            dma((blocks,)),
-            dma((blocks,)),
+            dma((units,)),
+            dma((units,)),
             dma((owners, sections)),
             dma(()),
             dma((n,)),
             dma((n,)),
             dma((sections,)),
             dma((sections,)),
+            pltpu.SemaphoreType.REGULAR,
         ],
         compiler_params=pltpu.CompilerParams(
             collective_id=0, has_side_effects=True, vmem_limit_bytes=60 * 1024 * 1024
         ),
-    )(step_sizes, cond, tokens.astype(BF16), own, embed, final, ada, up, down)
+    )(step_sizes, cond, tokens.astype(BF16).reshape(steps * patches, channels), own, embed, final, ada, up, down)
     return new_states.reshape(steps, batch, p_size // sections), errors[:steps, 0]
 
 

time: 148 us -> 145 us (0.980)
  Pallas kernels: 137 us -> 133 us
    pallas_call x1, Pallas kernels: 137 us -> 133 us  [shards(): pl.pallas_call(functools.partial(kernel, (n, groups, sections, width)), o...]
where the time goes in v1:
time: 145 us; the launch traced here: 144 us
  Pallas kernels  133 us (92%)
  local copies, waits for them, and re-layouts  6.84 us (5%)
  other arithmetic  3.4 us (2%)
    pallas_call x1, Pallas kernels, shards(): pl.pallas_call(functools.partial(kernel, (n, groups, sections, width)), o...  133 us

profile of v1, /device:TPU:27, one launch (start us, length us, event | category | flops | bytes accessed | tf_op | source)
XLA Modules:
  0.0 144.3 jit_solution(10129583328949543660)
XLA Ops:
  1.3 0.7 convert_element_type.30
  2.0 0.2 multiply_cosine_fusion
  2.1 0.1 pad_maximum_fusion
  2.2 0.1 concatenate.7
  2.3 0.8 convert_reduce_fusion.1
  3.0 0.1 reshape.122
  3.2 0.9 convert_reduce_fusion
  4.0 0.9 reduce.2
  4.9 0.6 pad.4.cond_ref
  5.5 0.8 convert_element_type.35.tokens_ref
  6.3 0.1 reshape.101
  6.5 0.6 constant_dynamic-slice_fusion.own_ref
  7.1 1.6 %copy.19.final_ref = bf16[1152,16]{1,0:T(8,128)(2,1)} copy(bf16[1152,16]{0,1:T(8,128)(2,1)} %param.19) | data formatting | bytes 73728 | tf_op args[9]
  8.7 132.7 %shard_map.113 = (f32[2,64,16]{2,1,0:T(8,128)}, f32[8,128]{1,0:T(8,128)}) custom-call(f32[2]{0:T(128)} %steps_ref.1, bf16[4,16,288]{2,1,0:T(8,128)(2,1)} %pad.4.cond_ref, bf16[512,16]{1,0:T(8,128)(2,1)} %convert_element_type.35.tokens_ref, f32[2,64,16]{2,1,0:T(8,128)} %constant_dynamic-slice_fusion.own_ref, bf16[16,1152]{1,0:T(8,128)(2,1)} %embed_ref.1, ...), custom_call_target="tpu_custom_call" | custom-call | tf_op jit(solution)/shard_map/pallas_call | solution.py:792
  141.5 1.5 %reshape.124 = f32[2,1,1024]{2,1,0:T(1,128)} reshape(f32[2,64,16]{2,1,0:T(8,128)} %get-tuple-element.4) | data formatting | bytes 16384 | tf_op jit(solution)/shard_map/reshape | solution.py:846
  143.0 1.3 slice_reduce_fusion
  (4 shorter events, 0.0 us)

commit v2 on v1

--- a/solution.py
+++ b/solution.py
@@ -13,6 +13,7 @@
 BF16 = jnp.bfloat16
 CORES = 2
 LAG = 2
+BEGIN = 5
 
 
 def round_up(value, to):
@@ -66,6 +67,14 @@
     down_full,
     condw,
     part,
+    flat,
+    scales,
+    scalew,
+    basis,
+    left,
+    lowpart,
+    loww,
+    lows,
     modw,
     first,
     hbuf,
@@ -102,6 +111,10 @@
     err_send,
     err_recv,
     go,
+    scale_send,
+    scale_recv,
+    low_send,
+    low_recv,
 ):
     n, groups, sections, width = cfg
     z = lax.axis_index("tm")
@@ -109,7 +122,7 @@
     s = lax.axis_index("section")
     steps = own_ref.shape[0]
     patches, channels = tokens_ref.shape[0] // steps, tokens_ref.shape[1]
-    wpad = final_ref.shape[0]
+    wpad = final_ref.shape[1]
     fpad = up_ref.shape[1]
 
     barrier = pltpu.get_barrier_semaphore()
@@ -266,11 +279,41 @@
 
     runs = [(w, members) for w in range(2) for members in sets]
     ahead = min(3, len(runs))
+    opening, early_waits = min(2, len(sets)), len(sets) - 1
+
+    count = len(sets)
+
+    def needs(at, act_on):
+        if at < count:
+            pl.when(s > 0)(act_on)
+        else:
+            act_on()
 
     def send_first():
-        for at, (w, members) in enumerate(runs):
-            if at < ahead:
-                own_sends(w, members, start)
+        @pl.when(s > 0)
+        def _():
+            for run in runs[:ahead]:
+                own_sends(*run, start)
+
+        @pl.when(s == 0)
+        def _():
+            own_sends(*runs[count], start)
+
+    def waits_early(at):
+        def act_on():
+            own_sends(*runs[at], wait_send)
+
+        pl.when((s > 0) if not count <= at < count + early_waits else s >= 0)(act_on)
+
+    def send_later(at):
+        if at < count + opening:
+
+            @pl.when(s > 0)
+            def _():
+                own_sends(*runs[at], start)
+
+        else:
+            own_sends(*runs[at], start)
 
     def relay(w, k, members):
         for case in range(groups):
@@ -338,6 +381,25 @@
     )
     for owner in range(n):
         part[owner] = products[owner * pad : owner * pad + steps]
+        flat[pl.ds(owner * steps, steps)] = products[owner * pad : owner * pad + steps, :wpad]
+    block = wpad // n
+    real = width // n
+
+    def scale_copy(k):
+        to = lax.rem(z + k, n)
+        return remote(
+            scales.at[to], scalew.at[z], scale_send.at[k - 1], scale_recv.at[k - 1], "tm", to
+        )
+
+    @pl.when(s == 0)
+    def _():
+        for owner in range(n):
+            scales[owner] = flat[:, owner * block : (owner + 1) * block]
+        for k in range(1, n):
+            scale_copy(k).start()
+        for run in runs[count + 1 : count + opening]:
+            own_sends(*run, start)
+        scalew[z] = scales[z]
 
     def slot_of(owner):
         return 0 if worker_of(owner, n) == owner else 1
@@ -368,6 +430,55 @@
         def _(owner=owner):
             modw[slot_of(owner), z] = part[owner]
 
+    def low_copy(owner):
+        slot = slot_of(owner)
+        return remote(
+            lowpart.at[owner],
+            loww.at[slot, z],
+            low_send.at[owner],
+            low_recv.at[slot, z],
+            "tm",
+            worker_of(owner, n),
+        )
+
+    def low_arrived(slot, source):
+        return remote(
+            loww.at[slot, source], loww.at[slot, source], low_send.at[0], low_recv.at[slot, source], "tm", z
+        )
+
+    @pl.when(s == 0)
+    def _():
+        embed = embed_ref[...].astype(F32)
+        embed = embed - jnp.sum(embed, axis=-1, keepdims=True) * (1.0 / width)
+        for owner in range(n):
+
+            @pl.when(z == owner)
+            def _(owner=owner):
+                basis[...] = embed[:, owner * block : (owner + 1) * block]
+
+        for k in range(1, n):
+            scale_copy(k).wait()
+        total = scalew[0]
+        for source in range(1, n):
+            total = total + scalew[source]
+        for row in range(n * steps):
+            left[pl.ds(row * channels, channels)] = (
+                basis[...] * (1.0 + total[row : row + 1])
+            ).astype(BF16)
+        group_rows = steps * channels
+        low = jnp.dot(left[...], up_ref[...], preferred_element_type=F32).astype(BF16)
+        for owner in range(n):
+            lowpart[owner] = low[owner * group_rows : (owner + 1) * group_rows]
+        for owner in range(n):
+
+            @pl.when(z != worker_of(owner, n))
+            def _(owner=owner):
+                low_copy(owner).start()
+
+            @pl.when(z == worker_of(owner, n))
+            def _(owner=owner):
+                loww[slot_of(owner), z] = lowpart[owner]
+
     @pl.when(jnp.logical_not(leads))
     def _():
         pl.semaphore_wait(go, 1)
@@ -375,24 +486,28 @@
 
     @pl.when(ends)
     def _():
-        for w, members in runs[ahead:]:
-            own_sends(w, members, start)
+        for at in range(ahead, len(runs)):
+            send_later(at)
 
     def release():
         pl.semaphore_signal(go, inc=1, device_id={"section": s + 1}, device_id_type=MESH)
 
-    block = wpad // n
-    real = width // n
     if block != real:
         mask = (lax.broadcasted_iota(jnp.int32, (1, wpad), 1) % block < real).astype(F32)
 
+    def centered(values):
+        center = values - jnp.sum(values, axis=-1, keepdims=True) * (1.0 / width)
+        return center * mask if block != real else center
+
+    def inverse_spread(center):
+        spread = jnp.sum(center * center, axis=-1, keepdims=True) * (1.0 / width)
+        return lax.rsqrt(spread + 1e-06)
+
     def normalize(values):
-        center = values - jnp.sum(values, axis=-1, keepdims=True) * (1.0 / width)
-        if block != real:
-            center = center * mask
-        spread = jnp.sum(center * center, axis=-1, keepdims=True) * (1.0 / width)
-        return center * lax.rsqrt(spread + 1e-06)
-
+        center = centered(values)
+        return center * inverse_spread(center)
+
+    tile = 256 if fpad % 256 == 0 else 128
     everything = pl.ds(0, units * span)
 
     def act_copy(u, at=None, rows=None):
@@ -420,31 +535,39 @@
         return (normalize(values) * (1.0 + mod[b, :, pl.ds(0, wpad)])).astype(BF16)
 
     def prepare():
-        @pl.when(s == 0)
-        def _():
-            tok[pl.ds(0, steps * patches)] = tokens_ref[...]
-            if paired:
-                patch_copy().wait_recv()
-
-        @pl.when(s > 0)
-        def _():
-            act_copy(0, rows=everything).wait_recv()
+        act_copy(0, rows=everything).wait_recv()
 
         def one(b, carry):
             rows = pl.ds(pl.multiple_of(b * patches, patches), patches)
-
-            @pl.when(s == 0)
-            def _():
-                hbuf[...] = jnp.dot(tok[rows], embed_ref[...], preferred_element_type=F32)
-
-            @pl.when(s > 0)
-            def _():
-                hbuf[...] = act[rows].astype(F32)
-
-            xbuf[rows] = scaled(b, hbuf[...])
+            xbuf[rows] = scaled(b, act[rows].astype(F32))
             return carry
 
         lax.fori_loop(0, blocks, one, 0)
+
+    def prepare_first():
+        tok[pl.ds(0, steps * patches)] = tokens_ref[...]
+        if paired:
+            patch_copy().wait_recv()
+        for slot in range(owners):
+            total = jnp.zeros(loww.shape[2:], F32)
+            for source in range(n):
+
+                @pl.when(z != source)
+                def _(slot=slot, source=source):
+                    low_arrived(slot, source).wait_recv()
+
+                total = total + loww[slot, source].astype(F32)
+            total = total.astype(BF16)
+            for step in range(steps):
+                lows[slot * steps + step] = total[step * channels : (step + 1) * channels]
+
+    def expand_first(b):
+        rows = pl.ds(b * patches, patches)
+        values = jnp.dot(tok[rows], embed_ref[...], preferred_element_type=F32)
+        inverse = inverse_spread(centered(values))
+        for at in range(0, fpad, tile):
+            inner = jnp.dot(tok[rows], lows[b, :, at : at + tile], preferred_element_type=F32)
+            ubuf[rows, at : at + tile] = gelu(inner * inverse)
 
     def columns_of(w, members):
         size = shard[w].shape[1] // pieces
@@ -486,49 +609,54 @@
                 act_copy(turn(i), at).start()
 
     streams = works & (s < early)
-    count = len(sets)
-    begin = min(3, 2 * count - 1)
+    begin = min(BEGIN, 2 * count - 1)
     behind = LAG * (last - 1) + 1
     expands = [max(j + behind, begin + 1 + j // 2) for j in range(count)]
-    tasks = [(begin, prepare, None)]
-    tasks += [(t, early_up, (0, members)) for t, members in zip(expands, sets)]
+    finish = len(runs) + LAG * (last - 1)
+    one, rest = streams & (s == 0), streams & (s > 0)
+    tasks = [(count + behind, one, prepare_first, None, ())]
+    tasks += [(count + behind + b, one, expand_first, None, (b,)) for b in range(blocks)]
+    tasks += [(finish, one, early_down, (1, members), (members,)) for members in sets]
+    tasks += [(begin, rest, prepare, None, ())]
+    tasks += [(t, rest, early_up, (0, members), (members,)) for t, members in zip(expands, sets)]
     tasks += [
-        (max(count + j + behind, expands[-1]), early_down, (1, members)) for j, members in enumerate(sets)
+        (max(count + j + behind, expands[-1]), rest, early_down, (1, members), (members,))
+        for j, members in enumerate(sets)
     ]
+    def settle(run, where):
+        pl.when(where)(lambda: rest_arrived(*run))
 
     def do(task):
-        _, work, run = task
+        _, where, work, run, given = task
         if run is not None:
-            rest_arrived(*run)
-
-        @pl.when(streams)
-        def _():
-            if run is None:
+            settle(run, (s == 0) if where is one else (s > 0))
+
+        @pl.when(where)
+        def _():
+            if work in (prepare, prepare_first):
                 modulations()
-                work()
-            else:
-                work(run[1])
+            work(*given)
 
     for w in range(2):
         local_copy(w).wait()
 
     @pl.when(led & ends)
     def _():
-        for w, members in runs[:-1]:
-            own_sends(w, members, wait_send)
+        for at in range(len(runs) - 1):
+            waits_early(at)
         release()
 
-    for t in range(len(runs) + LAG * (last - 1)):
+    for t in range(finish):
         if t + ahead < len(runs):
 
             @pl.when(jnp.logical_not(ends))
             def _(t=t):
-                own_sends(*runs[t + ahead], start)
+                send_later(t + ahead)
 
         for k in range(1, last + 1):
             if 0 <= t - LAG * (k - 1) < len(runs):
-                w, members = runs[t - LAG * (k - 1)]
-                relay(w, k, members)
+                at = t - LAG * (k - 1)
+                needs(at, lambda at=at, k=k: relay(runs[at][0], k, runs[at][1]))
         if t == len(runs) - 1:
 
             @pl.when(led & jnp.logical_not(ends))
@@ -539,7 +667,7 @@
             if task[0] == t:
                 do(task)
     for task in tasks:
-        if task[0] >= len(runs) + LAG * (last - 1):
+        if task[0] >= finish:
             do(task)
 
     @pl.when(streams & (s + 1 == early))
@@ -558,7 +686,16 @@
             device_id_type=MESH,
         )
 
-    tile = 256 if fpad % 256 == 0 else 128
+    def project(u):
+        rows = pl.ds(pl.multiple_of(u * span, span), span)
+        normed = normalize(leave[rows].astype(F32)).astype(BF16)
+        fresh = lax.dot_general(
+            normed, final_ref[...], (((1,), (1,)), ((), ())), preferred_element_type=F32
+        )
+        share = sections // cut
+        drift_all[pl.ds(lax.rem(u, cut) * share, share), u // cut] = fresh.reshape(
+            (share,) + drift_all.shape[2:]
+        )
 
     @pl.when(works & (s >= early))
     def _():
@@ -566,7 +703,7 @@
 
         def one(i, carry):
             u = turn(i)
-            b, part_of = u // cut, lax.rem(u, cut)
+            b = u // cut
             rows = pl.ds(pl.multiple_of(u * span, span), span)
             act_copy(u).wait_recv()
             x = scaled(b, act[rows].astype(F32))
@@ -580,29 +717,31 @@
             branch = jnp.dot(ubuf[rows], down_full[...], preferred_element_type=F32)
             result = (act[rows].astype(F32) + mod[b, :, pl.ds(wpad, wpad)] * branch).astype(BF16)
 
+            project(turn(jnp.maximum(i - 1, 0)))
+            leave[rows] = result
+
             @pl.when(s < sections - 1)
             def _():
-                leave[rows] = result
                 act_copy(u).start()
 
-            @pl.when(s == sections - 1)
-            def _():
-                normed = normalize(result.astype(F32)).astype(BF16)
-                fresh = jnp.dot(normed, final_ref[...], preferred_element_type=F32)
-                share = sections // cut
-                drift_all[pl.ds(part_of * share, share), b] = fresh.reshape(
-                    (share,) + drift_all.shape[2:]
-                )
-                for slot in range(owners):
-
-                    @pl.when(u == ((slot + 1) * steps) * cut - 1)
-                    def _(slot=slot):
-                        for d in range(sections if slot else sections - 1):
-                            drift_copy(slot, d).start()
+            if owners > 1:
+
+                @pl.when((s == sections - 1) & (i == steps * cut))
+                def _():
+                    for d in range(sections):
+                        drift_copy(1, d).start()
 
             return carry
 
+        first_rows = pl.ds(turn(0) * span, span)
+        leave[first_rows] = jnp.zeros((span, wpad), BF16)
         lax.fori_loop(0, units, one, 0)
+
+        @pl.when(s == sections - 1)
+        def _():
+            project(turn(units - 1))
+            for d in range(sections - 1):
+                drift_copy(0, d).start()
 
     here = works & (s == sections - 1)
 
@@ -679,16 +818,20 @@
 
     @pl.when(jnp.logical_not(led & ends))
     def _():
-        for w, members in runs[:-1]:
-            own_sends(w, members, wait_send)
-
-    for w, members in runs[-1:]:
-        own_sends(w, members, wait_send)
+        for at in range(len(runs) - 1):
+            needs(at, lambda at=at: own_sends(*runs[at], wait_send))
+
+    @pl.when(led & ends & (s == 0))
+    def _():
+        for at in range(count + early_waits, len(runs) - 1):
+            own_sends(*runs[at], wait_send)
+
+    own_sends(*runs[-1], wait_send)
     for w in range(2):
         for k in range(1, last + 1):
             for case in range(groups):
 
-                @pl.when(g == case)
+                @pl.when((g == case) if w else (g == case) & (s > 0))
                 def _(w=w, k=k, case=case):
                     for p in range(pieces):
                         if owner_of(w, p) == case:
@@ -715,6 +858,10 @@
         @pl.when(z != worker_of(owner, n))
         def _(owner=owner):
             mod_copy(owner).wait_send()
+
+            @pl.when(s == 0)
+            def _():
+                low_copy(owner).wait_send()
 
     if paired:
 
@@ -778,7 +925,7 @@
     tokens = states.reshape(steps, patches, channels)
     own = lax.dynamic_slice_in_dim(tokens, lax.axis_index("section") * own_patches, own_patches, 1)
     embed = pad_blocks(embed_weight, 1, n, block)
-    final = pad_blocks(final_weight, 0, n, block)
+    final = pad_blocks(final_weight.T, 1, n, block)
     ada = pad_blocks(ada_weight[0], 1, 2 * n, block)
     up = pad_blocks(pad_blocks(up_weight[0], 1, n, wide_block), 0, 1, block)
     down = pad_blocks(pad_blocks(down_weight[0], 1, n, block), 0, 1, wide_block)
@@ -802,6 +949,14 @@
             vmem((fpad, wpad), BF16),
             vmem((n, pad, width // n), BF16),
             vmem((n, steps, 2 * wpad), F32),
+            vmem((n * steps, wpad), F32),
+            vmem((n, n * steps, block), F32),
+            vmem((n, n * steps, block), F32),
+            vmem((channels, block), F32),
+            vmem((n * steps * channels, block), BF16),
+            vmem((n, steps * channels, fpad), BF16),
+            vmem((owners, n, steps * channels, fpad), BF16),
+            vmem((blocks, channels, fpad), BF16),
             vmem((owners, n, steps, 2 * wpad), F32),
             vmem(part_shape[1:], F32),
             vmem((patches, wpad), F32),
@@ -838,6 +993,10 @@
             dma((sections,)),
             dma((sections,)),
             pltpu.SemaphoreType.REGULAR,
+            dma((n,)),
+            dma((n,)),
+            dma((n,)),
+            dma((owners, n)),
         ],
         compiler_params=pltpu.CompilerParams(
             collective_id=0, has_side_effects=True, vmem_limit_bytes=60 * 1024 * 1024

time: 145 us -> 126 us (0.87)
  Pallas kernels: 133 us -> 116 us
  local copies, waits for them, and re-layouts: 6.84 us -> 5.18 us
    pallas_call x1, Pallas kernels: 133 us -> 116 us  [shards(): pl.pallas_call(functools.partial(kernel, (n, groups, sections, width)), o...]
    unnamed x2 -> x1, local copies, waits for them, and re-layouts: 1.65 us -> 0.01 us
where the time goes in v2:
time: 126 us
  Pallas kernels  116 us (92%)
  local copies, waits for them, and re-layouts  5.18 us (4%)
  other arithmetic  3.4 us (3%)
  between operations  1.32 us (1%)
    pallas_call x1, Pallas kernels, shards(): pl.pallas_call(functools.partial(kernel, (n, groups, sections, width)), o...  116 us

profile of v2, /device:TPU:27, one launch (start us, length us, event | category | flops | bytes accessed | tf_op | source)
XLA Modules:
  0.0 125.6 jit_solution(18079155675415471535)
XLA Ops:
  1.3 0.7 convert_reduce_fusion.1
  2.0 0.1 reshape.122
  2.1 0.7 convert_element_type.30
  2.8 0.2 multiply_cosine_fusion
  3.0 0.1 pad_maximum_fusion
  3.0 0.1 concatenate.7
  3.2 0.6 pad.4.cond_ref
  3.8 0.9 reduce.2
  4.6 0.1 reshape.101
  4.8 0.6 constant_dynamic-slice_fusion.own_ref
  5.4 0.9 convert_reduce_fusion
  6.3 0.8 convert_element_type.35.tokens_ref
  7.1 115.7 %shard_map.113 = (f32[2,64,16]{2,1,0:T(8,128)}, f32[8,128]{1,0:T(8,128)}) custom-call(f32[2]{0:T(128)} %steps_ref.1, bf16[4,16,288]{2,1,0:T(8,128)(2,1)} %pad.4.cond_ref, bf16[512,16]{1,0:T(8,128)(2,1)} %convert_element_type.35.tokens_ref, f32[2,64,16]{2,1,0:T(8,128)} %constant_dynamic-slice_fusion.own_ref, bf16[16,1152]{1,0:T(8,128)(2,1)} %embed_ref.1, ...), custom_call_target="tpu_custom_call" | custom-call | tf_op jit(solution)/shard_map/pallas_call | solution.py:939
  122.8 1.5 %reshape.124 = f32[2,1,1024]{2,1,0:T(1,128)} reshape(f32[2,64,16]{2,1,0:T(8,128)} %get-tuple-element.4) | data formatting | bytes 16384 | tf_op jit(solution)/shard_map/reshape | solution.py:1005
  124.3 1.3 %slice_reduce_fusion = f32[2]{0:T(128)} fusion(f32[8,128]{1,0:T(8,128)} %get-tuple-element.5), kind=kLoop, calls=%fused_computation.10 | loop fusion | bytes 16 | tf_op jit(solution)/shard_map/slice | solution.py:1005
  (4 shorter events, 0.0 us)

commit v3 on v2

--- a/solution.py
+++ b/solution.py
@@ -54,14 +54,13 @@
     cfg,
     steps_ref,
     cond_ref,
-    tokens_ref,
-    own_ref,
+    given_ref,
     embed_ref,
     final_ref,
     ada_ref,
     up_ref,
     down_ref,
-    new_ref,
+    out_ref,
     err_ref,
     up_full,
     down_full,
@@ -115,13 +114,21 @@
     scale_recv,
     low_send,
     low_recv,
+    new_ref,
+    states_ref,
 ):
     n, groups, sections, width = cfg
     z = lax.axis_index("tm")
     g = lax.axis_index("groups")
     s = lax.axis_index("section")
-    steps = own_ref.shape[0]
-    patches, channels = tokens_ref.shape[0] // steps, tokens_ref.shape[1]
+    steps, patches, channels = states_ref.shape
+    lanes = given_ref.shape[2] // channels
+    for b in range(steps):
+        for j in range(lanes):
+            states_ref[b, pl.ds(j, given_ref.shape[1], stride=lanes), :] = given_ref[
+                b, :, j * channels : (j + 1) * channels
+            ]
+    held = patches // sections
     wpad = final_ref.shape[1]
     fpad = up_ref.shape[1]
 
@@ -174,17 +181,30 @@
     for k in range(1, n):
         cond_copy(k).start()
 
+    def own(b):
+        return states_ref.at[b, pl.ds(pl.multiple_of(s * held, held), held)]
+
     def first_copy(k):
-        return remote(own_ref.at[0], first, first_send.at[k - 1], first_recv, "tm", k)
+        return remote(own(0), first, first_send.at[k - 1], first_recv, "tm", k)
 
     @pl.when(z == 0)
     def _():
         for k in range(1, n):
             first_copy(k).start()
 
+    @pl.when(s == 0)
+    def _():
+        for b in range(steps):
+            tok[pl.ds(b * patches, patches)] = states_ref[b].astype(BF16)
+
     def patch_copy():
         return remote(
-            tokens_ref, tok.at[pl.ds(steps * patches, steps * patches)], patch_send, patch_recv, "tm", inward
+            tok.at[pl.ds(0, steps * patches)],
+            tok.at[pl.ds(steps * patches, steps * patches)],
+            patch_send,
+            patch_recv,
+            "tm",
+            inward,
         )
 
     if paired:
@@ -545,7 +565,6 @@
         lax.fori_loop(0, blocks, one, 0)
 
     def prepare_first():
-        tok[pl.ds(0, steps * patches)] = tokens_ref[...]
         if paired:
             patch_copy().wait_recv()
         for slot in range(owners):
@@ -769,7 +788,7 @@
 
     @pl.when(z == 0)
     def _():
-        first[...] = own_ref[0]
+        first[...] = own(0)[...]
 
     @pl.when(z > 0)
     def _():
@@ -791,10 +810,14 @@
         fresh = base + running
         running = running + steps_ref[b] * drift[b]
         new_ref[b] = fresh
-        delta = jnp.max(jnp.abs(fresh - own_ref[b]), axis=0, keepdims=True)
+        delta = jnp.max(jnp.abs(fresh - own(b)[...]), axis=0, keepdims=True)
         errors.append(jnp.broadcast_to(jnp.max(delta, axis=1, keepdims=True), (1, 128)))
     for b in range(steps):
         err_own[pl.ds(b, 1), :] = errors[b]
+    for b in range(steps):
+        out_ref[b] = jnp.concatenate(
+            [new_ref[b, pl.ds(j, out_ref.shape[1], stride=lanes), :] for j in range(lanes)], axis=1
+        )
     for b in range(steps, err_own.shape[0]):
         err_own[pl.ds(b, 1), :] = jnp.zeros((1, 128), F32)
 
@@ -922,8 +945,7 @@
 
     cond = condition_rows(timesteps, labels, class_table).reshape(steps, n, width // n)
     cond = jnp.pad(cond.transpose(1, 0, 2), ((0, 0), (0, pad - steps), (0, 0)))
-    tokens = states.reshape(steps, patches, channels)
-    own = lax.dynamic_slice_in_dim(tokens, lax.axis_index("section") * own_patches, own_patches, 1)
+    tokens = states.reshape(steps, p_size // 128, 128)
     embed = pad_blocks(embed_weight, 1, n, block)
     final = pad_blocks(final_weight.T, 1, n, block)
     ada = pad_blocks(ada_weight[0], 1, 2 * n, block)
@@ -939,10 +961,10 @@
     new_states, errors = pl.pallas_call(
         functools.partial(kernel, (n, groups, sections, width)),
         out_shape=(
-            jax.ShapeDtypeStruct(part_shape, F32),
+            jax.ShapeDtypeStruct((steps, own_patches * channels // 128, 128), F32),
             jax.ShapeDtypeStruct((8, 128), F32),
         ),
-        in_specs=[pl.BlockSpec(memory_space=pltpu.SMEM)] + [pl.BlockSpec(memory_space=vmem)] * 8,
+        in_specs=[pl.BlockSpec(memory_space=pltpu.SMEM)] + [pl.BlockSpec(memory_space=vmem)] * 7,
         out_specs=(pl.BlockSpec(memory_space=vmem), pl.BlockSpec(memory_space=vmem)),
         scratch_shapes=[
             vmem((wpad, fpad), BF16),
@@ -997,11 +1019,13 @@
             dma((n,)),
             dma((n,)),
             dma((owners, n)),
+            vmem(part_shape, F32),
+            vmem((steps, patches, channels), F32),
         ],
         compiler_params=pltpu.CompilerParams(
             collective_id=0, has_side_effects=True, vmem_limit_bytes=60 * 1024 * 1024
         ),
-    )(step_sizes, cond, tokens.astype(BF16).reshape(steps * patches, channels), own, embed, final, ada, up, down)
+    )(step_sizes, cond, tokens, embed, final, ada, up, down)
     return new_states.reshape(steps, batch, p_size // sections), errors[:steps, 0]
 
 

time: 126 us -> 123 us (0.976)
  local copies, waits for them, and re-layouts: 5.18 us -> 3.4 us
  other arithmetic: 3.4 us -> 1.69 us
    reshape x2 -> x0, local copies, waits for them, and re-layouts: 1.66 us -> none  [the longest x1 1.53 us: shards(): new_states.reshape(steps, batch, p_size // sections)]
    unnamed x1 -> x2, local copies, waits for them, and re-layouts: 0.01 us -> 1.3 us
where the time goes in v3:
time: 123 us; the launch traced here: 122 us
  Pallas kernels  116 us (94%)
  local copies, waits for them, and re-layouts  3.4 us (3%)
  other arithmetic  1.69 us (1%)
  between operations  1.31 us (1%)
    pallas_call x1, Pallas kernels, shards(): pl.pallas_call(functools.partial(kernel, (n, groups, sections, width)), o...  116 us

profile of v3, /device:TPU:27, one launch (start us, length us, event | category | flops | bytes accessed | tf_op | source)
XLA Modules:
  0.0 122.3 jit_solution(10380301385454731001)
XLA Ops:
  1.3 0.7 convert_element_type.23
  1.9 0.2 multiply_cosine_fusion
  2.1 0.1 pad_maximum_fusion
  2.2 0.1 concatenate.7
  2.3 0.8 convert_reduce_fusion
  3.0 0.1 reshape.119
  3.2 0.6 pad.4.cond_ref
  3.8 115.9 %shard_map.113 = (f32[2,8,128]{2,1,0:T(8,128)}, f32[8,128]{1,0:T(8,128)}) custom-call(f32[2]{0:T(128)} %steps_ref.1, bf16[4,16,288]{2,1,0:T(8,128)(2,1)} %pad.4.cond_ref, f32[2,32,128]{2,1,0:T(8,128)} %bitcast.21, bf16[16,1152]{1,0:T(8,128)(2,1)} %embed_ref.1, bf16[16,1152]{1,0:T(8,128)(2,1)} %bitcast.20, bf16[288,2304]{1,0:T(8,128)(2,1)} %bitcast.14, ...), custom_call_target="tpu_custom_call" | custom-call | tf_op jit(solution)/shard_map/pallas_call | solution.py:961
  119.7 1.3 %slice_reduce_fusion = f32[2]{0:T(128)} fusion(f32[8,128]{1,0:T(8,128)} %get-tuple-element.5), kind=kLoop, calls=%fused_computation.9 | loop fusion | bytes 16 | tf_op jit(solution)/shard_map/slice | solution.py:1029
  121.0 1.3 %copy.25 = f32[2,1,1024]{2,1,0:T(1,128)} copy(f32[2,1,1024]{2,1,0:T(1,128)} %bitcast.22) | data formatting | bytes 16384
  (4 shorter events, 0.0 us)
